TPU v7x, 16 devices: a whole 2x2x2 slice. The times are simulated.
16 devices in a mesh: dp: 4 (over z, y), sp: 4 (over x, core).
Axes of the slice: x: 2, y: 2, z: 2, core: 2. Of those that a mesh axis runs over, the one named last changes fastest.
Arguments:
- patches: bfloat16 [8, 3072, 1536], P('dp', 'sp'), parts along dimension 0
- vis_mask: int32 [8, 3072], P('dp', 'sp'), parts along dimension 0
- enc_pos: bfloat16 [12288, 768], P(('dp', 'sp')), parts along dimension 0
- dec_pos: bfloat16 [12288, 384], P(('dp', 'sp')), parts along dimension 0
- w_pe: bfloat16 [1536, 768], replicated
- b_pe: bfloat16 [768], replicated
- enc_qkv: bfloat16 [2, 768, 3, 12, 64], replicated
- enc_proj: bfloat16 [2, 12, 64, 768], replicated
- enc_up: bfloat16 [2, 768, 3072], replicated
- enc_down: bfloat16 [2, 3072, 768], replicated
- w_ed: bfloat16 [768, 384], replicated
- mask_token: bfloat16 [384], replicated
- dec_qkv: bfloat16 [2, 384, 3, 6, 64], replicated
- dec_proj: bfloat16 [2, 6, 64, 384], replicated
- dec_up: bfloat16 [2, 384, 1536], replicated
- dec_down: bfloat16 [2, 1536, 384], replicated
- w_out: bfloat16 [384, 1536], replicated
Outputs:
- output: float32 [8, 3072, 1536], P('dp', 'sp'), parts along dimension 0
There are 4 independent parts. A program takes and returns all parts, laid end to end along the dimension named above; an argument that names none is the same for every part.
All inputs are finite; a program needn't handle non-finite values.
Results may differ from a plain program's by a relative error of at most 0.0157076.
Values are sent between devices in bfloat16 or wider.
A program may use at most 1 GiB of HBM per device.

v0:
```python
import jax
import jax.numpy as jnp
from jax import lax
from jax.sharding import PartitionSpec as P

KEEP_DIV = 8


def layer_norm(hidden):
    hid_f32 = hidden.astype(jnp.float32)
    centred = hid_f32 - jnp.mean(hid_f32, axis=-1, keepdims=True)
    row_var = jnp.mean(centred * centred, axis=-1, keepdims=True)
    return (centred * lax.rsqrt(row_var + 1e-6)).astype(jnp.bfloat16)


def attn_mlp_block(hidden, w_qkv, w_proj, w_up, w_down):
    proj_qkv = jnp.einsum('cnd,dshk->scnhk', layer_norm(hidden), w_qkv, preferred_element_type=jnp.float32).astype(jnp.bfloat16)
    kv_all = lax.all_gather(proj_qkv[1:], 'sp', axis=2, tiled=True)
    scores = jnp.einsum('cqhk,cshk->chqs', proj_qkv[0], kv_all[0], preferred_element_type=jnp.float32) * proj_qkv.shape[-1] ** -0.5
    attn_probs = jax.nn.softmax(scores, axis=-1).astype(jnp.bfloat16)
    attended = jnp.einsum('chqs,cshk->cqhk', attn_probs, kv_all[1], preferred_element_type=jnp.float32).astype(jnp.bfloat16)
    mid_state = (hidden + jnp.einsum('cqhk,hkd->cqd', attended, w_proj, preferred_element_type=jnp.float32)).astype(jnp.bfloat16)
    up_act = jax.nn.gelu(jnp.einsum('cnd,df->cnf', layer_norm(mid_state), w_up, preferred_element_type=jnp.float32), approximate=False).astype(jnp.bfloat16)
    return (mid_state + jnp.einsum('cnf,fd->cnd', up_act, w_down, preferred_element_type=jnp.float32)).astype(jnp.bfloat16)


def solution(mesh):
    group_size = mesh.shape['sp']
    to_next = [(src_dev, src_dev + 1) for src_dev in range(group_size - 1)]
    to_prev = [(src_dev + 1, src_dev) for src_dev in range(group_size - 1)]

    def local_program(patches, vis_mask, enc_pos, dec_pos, w_pe, b_pe, enc_qkv, enc_proj, enc_up, enc_down, w_ed, mask_token, dec_qkv, dec_proj, dec_up, dec_down, w_out):
        vis_shard = patches.shape[1] // KEEP_DIV
        half_rows = vis_shard // 2
        my_index = lax.axis_index('sp')
        vis_counts = lax.all_gather(jnp.sum(vis_mask, axis=1), 'sp')
        vis_before = jnp.sum(jnp.where(jnp.arange(group_size)[:, None] < my_index, vis_counts, 0), axis=0)
        local_rank = jnp.cumsum(vis_mask, axis=1) - vis_mask
        dest_row = vis_before[:, None] + local_rank - my_index * vis_shard + half_rows
        row_ids = jnp.arange(2 * vis_shard)
        select = ((dest_row[:, None, :] == row_ids[None, :, None]) & (vis_mask[:, None, :] == 1)).astype(jnp.bfloat16)
        moved_x = jnp.einsum('cqi,cip->cqp', select, patches, preferred_element_type=jnp.float32).astype(jnp.bfloat16)
        moved_pos = jnp.einsum('cqi,id->cqd', select, enc_pos, preferred_element_type=jnp.float32)
        occupied = jnp.sum(select, axis=2, dtype=jnp.float32)
        embedded = (jnp.einsum('cqp,pd->cqd', moved_x, w_pe, preferred_element_type=jnp.float32)
                    + occupied[:, :, None] * b_pe.astype(jnp.float32) + moved_pos).astype(jnp.bfloat16)
        from_prev = lax.ppermute(embedded[:, 3 * half_rows:], 'sp', to_next)
        from_next = lax.ppermute(embedded[:, :half_rows], 'sp', to_prev)
        hidden = embedded[:, half_rows:3 * half_rows] + jnp.concatenate([from_prev, from_next], axis=1)
        for layer_idx in range(enc_qkv.shape[0]):
            hidden = attn_mlp_block(hidden, enc_qkv[layer_idx], enc_proj[layer_idx], enc_up[layer_idx], enc_down[layer_idx])
        z_enc = jnp.einsum('cnd,de->cne', layer_norm(hidden), w_ed, preferred_element_type=jnp.float32).astype(jnp.bfloat16)
        z_prev = lax.ppermute(z_enc[:, half_rows:], 'sp', to_next)
        z_next = lax.ppermute(z_enc[:, :half_rows], 'sp', to_prev)
        z_rows = jnp.concatenate([z_prev, z_enc, z_next], axis=1)
        placed = jnp.einsum('cqi,cqe->cie', select, z_rows, preferred_element_type=jnp.float32)
        masked_part = (1 - vis_mask).astype(jnp.float32)[:, :, None] * mask_token.astype(jnp.float32)
        hidden = (placed + masked_part + dec_pos.astype(jnp.float32)).astype(jnp.bfloat16)
        for layer_idx in range(dec_qkv.shape[0]):
            hidden = attn_mlp_block(hidden, dec_qkv[layer_idx], dec_proj[layer_idx], dec_up[layer_idx], dec_down[layer_idx])
        return jnp.einsum('cne,ep->cnp', layer_norm(hidden), w_out, preferred_element_type=jnp.float32)

    row_spec = P('dp', 'sp', None)
    pos_spec = P(('dp', 'sp'), None)
    arg_specs = (row_spec, P('dp', 'sp'), pos_spec, pos_spec) + (P(),) * 13
    return jax.shard_map(local_program, mesh=mesh, in_specs=arg_specs, out_specs=row_spec, check_vma=False)
```

profile of v0, /device:TPU:0, one launch (start us, length us, event | category | flops | bytes accessed | tf_op | source)
XLA Modules:
  0.0 588.3 jit_solution(12771200385057387067)
XLA Ops:
  11.1 6.6 %all-reduce = s32[8]{0:T(128)S(1)} all-reduce(s32[8]{0:T(128)S(1)} %dynamic-update-slice), channel_id=2, replica_groups=mesh['dp'=4,'sp'=4] {'sp'}, use_global_device_ids=true, to_apply=%add | all-reduce | flops 8 | bytes 64
  20.9 4.3 fusion.97
  37.2 39.0 %all-gather.6.cloned.1.call-done = bf16[2,2,384,12,64]{4,1,3,0,2:T(2,128)(2,1)} async-done(((bf16[2,2,96,12,64]{4,1,3,0,2:T(2,128)(2,1)}), bf16[2,2,384,12,64]{4,1,3,0,2:T(2,128)(2,1)}) %all-gather.6.cloned.1.call-update) | async-done | bytes 2359312 | tf_op jit(solution)/shard_map/all_gather | solution.py:18
  76.3 7.0 %fusion.498 = (bf16[1,2,384,12,64]{4,1,3,0,2:T(2,128)(2,1)}, bf16[1,2,384,12,64]{4,1,3,0,2:T(2,128)(2,1)S(1)}) fusion(bf16[2,2,384,12,64]{4,1,3,0,2:T(2,128)(2,1)} %all-gather.6.cloned.1.call-done), kind=kLoop, calls=%fused_computation.553 | loop fusion | bytes 4718592 | tf_op jit(solution)/shard_map/slice | solution.py:21
  83.3 7.0 %copy.63 = bf16[1,2,384,12,64]{2,4,3,1,0:T(8,128)(2,1)} copy(bf16[1,2,384,12,64]{4,1,3,0,2:T(2,128)(2,1)} %get-tuple-element.17) | data formatting | bytes 2359296
  97.2 8.1 %fusion.502 = (f32[2,96]{1,0:T(2,128)S(1)}, f32[2,96,768]{2,1,0:T(8,128)S(1)}) fusion(bf16[2,12,64,768]{3,2,1,0:T(8,128)(2,1)} %param.24, f32[2,12,96]{2,1,0:T(8,128)S(1)} %fusion.501, bf16[1,2,384,12,64]{2,4,3,1,0:T(8,128)(2,1)S(1)} %copy-done.7, f32[2,12,96,384]{3,2,1,0:T(8,128)} %copy-done.2, bf16[2,96,768]{2,1,0:T(8,128)(2,1)S(1)} %copy-done.16), kind=kOutput, calls=%fused_computation.557 | convolution fusion | flops 345049536 | bytes 10331904 | tf_op jit(solution)/shard_map/cqhk,hkd->cqd/dot_general | solution.py:22
  105.6 4.3 fusion.309
  109.9 8.2 %fusion.507 = (f32[2,96]{1,0:T(2,128)S(1)}, f32[2,96,768]{2,1,0:T(8,128)S(1)}) fusion(f32[2,96,768]{2,1,0:T(8,128)S(1)} %get-tuple-element.26, bf16[2,3072,768]{2,1,0:T(8,128)(2,1)} %param.26, f32[2,96,3072]{2,1,0:T(8,128)S(1)} %get-tuple-element.27, u8[96,3072]{1,0:T(8,128)(4,1)S(1)} %get-tuple-element.12, u8[96,3072]{1,0:T(8,128)(4,1)S(1)} %get-tuple-element.11), kind=kOutput, calls=%fused_computation.558 | convolution fusion | flops 947846976 | bytes 8848128 | tf_op jit(solution)/shard_map/cnf,fd->cnd/dot_general | solution.py:24
  122.5 35.4 %all-gather.8.cloned.1.call-done = bf16[2,2,384,12,64]{4,1,3,0,2:T(2,128)(2,1)} async-done(((bf16[2,2,96,12,64]{4,1,3,0,2:T(2,128)(2,1)}), bf16[2,2,384,12,64]{4,1,3,0,2:T(2,128)(2,1)}) %all-gather.8.cloned.1.call-update) | async-done | bytes 2359312 | tf_op jit(solution)/shard_map/all_gather | solution.py:18
  157.9 7.0 %fusion.497 = (bf16[1,2,384,12,64]{4,1,3,0,2:T(2,128)(2,1)}, bf16[1,2,384,12,64]{4,1,3,0,2:T(2,128)(2,1)S(1)}) fusion(bf16[2,2,384,12,64]{4,1,3,0,2:T(2,128)(2,1)} %all-gather.8.cloned.1.call-done), kind=kLoop, calls=%fused_computation.552 | loop fusion | bytes 4718592 | tf_op jit(solution)/shard_map/slice | solution.py:21
  164.9 6.5 %copy.65 = bf16[1,2,384,12,64]{2,4,3,1,0:T(8,128)(2,1)} copy(bf16[1,2,384,12,64]{4,1,3,0,2:T(2,128)(2,1)} %get-tuple-element.15) | data formatting | bytes 2359296
  178.4 8.1 %fusion.509 = (f32[2,96]{1,0:T(2,128)S(1)}, f32[2,96,768]{2,1,0:T(8,128)S(1)}) fusion(f32[2,96,768]{2,1,0:T(8,128)S(1)} %copy-done.20, bf16[2,12,64,768]{3,2,1,0:T(8,128)(2,1)} %param.24, f32[2,12,96]{2,1,0:T(8,128)S(1)} %fusion.508, bf16[1,2,384,12,64]{2,4,3,1,0:T(8,128)(2,1)S(1)} %copy-done.8, f32[2,12,96,384]{3,2,1,0:T(8,128)} %copy-done.3), kind=kOutput, calls=%fused_computation.560 | convolution fusion | flops 344902080 | bytes 10626816 | tf_op jit(solution)/shard_map/cqhk,hkd->cqd/dot_general | solution.py:22
  190.9 8.1 %fusion.514 = (f32[2,96]{1,0:T(2,128)S(1)}, f32[2,96,768]{2,1,0:T(8,128)S(1)}) fusion(f32[2,96,768]{2,1,0:T(8,128)S(1)} %get-tuple-element.31, bf16[2,3072,768]{2,1,0:T(8,128)(2,1)} %param.26, f32[2,96,3072]{2,1,0:T(8,128)S(1)} %get-tuple-element.32, u8[96,3072]{1,0:T(8,128)(4,1)S(1)} %get-tuple-element.10, u8[96,3072]{1,0:T(8,128)(4,1)S(1)} %get-tuple-element.9), kind=kOutput, calls=%fused_computation.561 | convolution fusion | flops 947846976 | bytes 8848128 | tf_op jit(solution)/shard_map/cnf,fd->cnd/dot_general | solution.py:24
  212.0 65.4 %all-gather.10.cloned.1.call-done = bf16[2,2,3072,6,64]{2,4,3,0,1:T(8,128)(2,1)} async-done(((bf16[2,2,768,6,64]{2,4,3,0,1:T(8,128)(2,1)}), bf16[2,2,3072,6,64]{2,4,3,0,1:T(8,128)(2,1)}) %all-gather.10.cloned.1.call-update) | async-done | bytes 9437200 | tf_op jit(solution)/shard_map/all_gather | solution.py:18
  277.4 44.4 %fusion.515 = (f32[2,6,768]{2,1,0:T(8,128)S(1)}, f32[2,6,768,3072]{3,2,1,0:T(8,128)}) fusion(bf16[2,2,3072,6,64]{2,4,3,0,1:T(8,128)(2,1)} %all-gather.10.cloned.1.call-done, bf16[3,2,768,6,64]{2,4,3,0,1:T(8,128)(2,1)} %copy-done.4), kind=kOutput, calls=%fused_computation.562 | convolution fusion | flops 3708816384 | bytes 119181312 | tf_op jit(solution)/shard_map/sub | solution.py:20
  321.8 39.4 %fusion.142 = bf16[2,768,6,64]{1,3,2,0:T(8,128)(2,1)} fusion(f32[2,6,768,3072]{3,2,1,0:T(8,128)} %get-tuple-element.38, f32[2,6,768]{2,1,0:T(8,128)S(1)} %get-tuple-element.37, bf16[2,2,3072,6,64]{2,4,3,0,1:T(8,128)(2,1)} %all-gather.10.cloned.1.call-done), kind=kOutput, calls=%fused_computation.202 | convolution fusion | flops 3681091584 | bytes 119181312 | tf_op jit(solution)/shard_map/chqs,cshk->cqhk/dot_general | solution.py:21
  363.9 5.3 fusion.113
  369.2 23.1 %convert_reduce_fusion.1 = (f32[2,768]{1,0:T(2,128)S(1)}, bf16[2,768,384]{1,2,0:T(8,128)(2,1)S(1)}) fusion(bf16[2,1536,384]{2,1,0:T(8,128)(2,1)S(1)} %copy-done.26, f32[2,768,1536]{2,1,0:T(8,128)S(1)} %get-tuple-element.41, u8[768,1536]{1,0:T(8,128)(4,1)S(1)} %get-tuple-element.8, u8[768,1536]{1,0:T(8,128)(4,1)S(1)} %get-tuple-element.7, ...), kind=kOutput, calls=%fused_computation.99 | convolution fusion | flops 1980037632 | bytes 15341568 | tf_op jit(solution)/shard_map/cnf,fd->cnd/dot_general | solution.py:24
  398.1 62.8 %all-gather.12.cloned.1.call-done = bf16[2,2,3072,6,64]{2,4,3,0,1:T(8,128)(2,1)} async-done(((bf16[2,2,768,6,64]{2,4,3,0,1:T(8,128)(2,1)}), bf16[2,2,3072,6,64]{2,4,3,0,1:T(8,128)(2,1)}) %all-gather.12.cloned.1.call-update) | async-done | bytes 9437200 | tf_op jit(solution)/shard_map/all_gather | solution.py:18
  461.0 44.5 %fusion.516 = (f32[2,6,768]{2,1,0:T(8,128)S(1)}, f32[2,6,768,3072]{3,2,1,0:T(8,128)}) fusion(bf16[2,2,3072,6,64]{2,4,3,0,1:T(8,128)(2,1)} %all-gather.12.cloned.1.call-done, bf16[3,2,768,6,64]{2,4,3,0,1:T(8,128)(2,1)} %copy-done.5), kind=kOutput, calls=%fused_computation.563 | convolution fusion | flops 3708816384 | bytes 119181312 | tf_op jit(solution)/shard_map/sub | solution.py:20
  505.5 39.4 %fusion.143 = bf16[2,768,6,64]{1,3,2,0:T(8,128)(2,1)} fusion(f32[2,6,768,3072]{3,2,1,0:T(8,128)} %get-tuple-element.45, f32[2,6,768]{2,1,0:T(8,128)S(1)} %get-tuple-element.44, bf16[2,2,3072,6,64]{2,4,3,0,1:T(8,128)(2,1)} %all-gather.12.cloned.1.call-done), kind=kOutput, calls=%fused_computation.203 | convolution fusion | flops 3681091584 | bytes 119181312 | tf_op jit(solution)/shard_map/chqs,cshk->cqhk/dot_general | solution.py:21
  547.6 5.3 fusion.114
  552.9 23.1 %convert_reduce_fusion.4 = (f32[2,768]{1,0:T(2,128)S(1)}, bf16[2,768,384]{1,2,0:T(8,128)(2,1)S(1)}) fusion(bf16[2,1536,384]{2,1,0:T(8,128)(2,1)S(1)} %copy-done.27, f32[2,768,1536]{2,1,0:T(8,128)S(1)} %get-tuple-element.48, u8[768,1536]{1,0:T(8,128)(4,1)S(1)} %get-tuple-element.6, u8[768,1536]{1,0:T(8,128)(4,1)S(1)} %get-tuple-element.5, ...), kind=kOutput, calls=%fused_computation.113 | convolution fusion | flops 1980037632 | bytes 15341568 | tf_op jit(solution)/shard_map/cnf,fd->cnd/dot_general | solution.py:24
  576.4 5.2 fusion.175
  (158 shorter events, 65.8 us)
Async XLA Ops:
  6.5 14.4 %copy-start = (bf16[1536,768]{1,0:T(8,128)(2,1)S(1)}, bf16[1536,768]{1,0:T(8,128)(2,1)}, u32[]{:S(2)}) copy-start(bf16[1536,768]{1,0:T(8,128)(2,1)} %param.21) | copy-start | bytes 7077892
  6.5 69.7 %all-gather.6.cloned.1.call-start = ((), (), s32[]{:S(2)}) async-start(), calls=%async_computation | async-start | bytes 5898240 | tf_op jit(solution)/shard_map/all_gather | solution.py:18
  25.2 8.5 %copy-start.23 = (bf16[2,768,3,12,64]{1,4,3,2,0:T(8,128)(2,1)S(1)}, bf16[2,768,3,12,64]{1,4,3,2,0:T(8,128)(2,1)}, u32[]{:S(2)}) copy-start(bf16[2,768,3,12,64]{1,4,3,2,0:T(8,128)(2,1)} %param.23) | copy-start | bytes 21233668
  27.7 2.6 collective-permute-start
  29.0 4.4 collective-permute-start.1
  37.2 120.7 %all-gather.8.cloned.1.call-start = ((), (), s32[]{:S(2)}) async-start(), calls=%async_computation.1 | async-start | bytes 5898240 | tf_op jit(solution)/shard_map/all_gather | solution.py:18
  105.5 13.4 %slice-start = ((s8[7077888]{0:T(1024)(128)(4,1)}), s8[2883584]{0:T(1024)(128)(4,1)S(1)}, s32[]{:S(2)}) async-start(s8[7077888]{0:T(1024)(128)(4,1)} %bitcast.293), calls=%async_computation.4 | async-start | bytes 5767168
  109.9 9.0 %slice-start.1 = ((s8[7077888]{0:T(1024)(128)(4,1)}), s8[4194304]{0:T(1024)(128)(4,1)S(1)}, s32[]{:S(2)}) async-start(s8[7077888]{0:T(1024)(128)(4,1)} %bitcast.293), calls=%async_computation.5 | async-start | bytes 8388608
  122.3 155.1 %all-gather.10.cloned.1.call-start = ((), (), s32[]{:S(2)}) async-start(), calls=%async_computation.2 | async-start | bytes 11796480 | tf_op jit(solution)/shard_map/all_gather | solution.py:18
  190.9 8.4 %copy-start.18 = (bf16[768,384]{1,0:T(8,128)(2,1)S(1)}, bf16[768,384]{1,0:T(8,128)(2,1)}, u32[]{:S(2)}) copy-start(bf16[768,384]{1,0:T(8,128)(2,1)} %param.27) | copy-start | bytes 1769476
  190.9 12.7 %copy-start.22 = (bf16[384]{0:T(512)(128)(2,1)S(1)}, bf16[384]{0:T(512)(128)(2,1)}, u32[]{:S(2)}) copy-start(bf16[384]{0:T(512)(128)(2,1)} %param.28) | copy-start | bytes 2308
  199.1 6.0 %copy-start.21 = (f32[2,768]{1,0:T(2,128)S(1)}, f32[2,768]{1,0:T(2,128)}, u32[]{:S(2)}) copy-start(f32[2,768]{1,0:T(2,128)} %get-tuple-element.24) | copy-start | bytes 18436
  199.7 4.1 collective-permute-start.2
  201.9 3.2 collective-permute-start.3
  212.0 249.0 %all-gather.12.cloned.1.call-start = ((), (), s32[]{:S(2)}) async-start(), calls=%async_computation.3 | async-start | bytes 11796480 | tf_op jit(solution)/shard_map/all_gather | solution.py:18
  321.8 39.4 %copy-start.12 = (bf16[2,768,384]{1,2,0:T(8,128)(2,1)S(1)}, bf16[2,768,384]{1,2,0:T(8,128)(2,1)}, u32[]{:S(2)}) copy-start(bf16[2,768,384]{1,2,0:T(8,128)(2,1)} %copy-done.11) | copy-start | bytes 3538948
  321.8 39.4 %copy-start.30 = (bf16[2,6,64,384]{3,2,1,0:T(8,128)(2,1)S(1)}, bf16[2,6,64,384]{3,2,1,0:T(8,128)(2,1)}, u32[]{:S(2)}) copy-start(bf16[2,6,64,384]{3,2,1,0:T(8,128)(2,1)} %param.30) | copy-start | bytes 1769476
  363.8 5.3 copy-start.26
  369.2 23.5 %copy-start.29 = (bf16[2,384,3,6,64]{1,4,3,2,0:T(8,128)(2,1)S(1)}, bf16[2,384,3,6,64]{1,4,3,2,0:T(8,128)(2,1)}, u32[]{:S(2)}) copy-start(bf16[2,384,3,6,64]{1,4,3,2,0:T(8,128)(2,1)} %param.29) | copy-start | bytes 5308420
  505.5 39.4 %copy-start.14 = (bf16[2,768,384]{1,2,0:T(8,128)(2,1)S(1)}, bf16[2,768,384]{1,2,0:T(8,128)(2,1)}, u32[]{:S(2)}) copy-start(bf16[2,768,384]{1,2,0:T(8,128)(2,1)} %copy-done.13) | copy-start | bytes 3538948
  505.5 39.4 %copy-start.31 = (bf16[2,6,64,384]{3,2,1,0:T(8,128)(2,1)S(1)}, bf16[2,6,64,384]{3,2,1,0:T(8,128)(2,1)}, u32[]{:S(2)}) copy-start(bf16[2,6,64,384]{3,2,1,0:T(8,128)(2,1)} %param.30) | copy-start | bytes 1769476
  547.6 5.3 copy-start.27
  552.9 23.5 %copy-start.6 = (bf16[384,1536]{1,0:T(8,128)(2,1)S(1)}, bf16[384,1536]{1,0:T(8,128)(2,1)}, u32[]{:S(2)}) copy-start(bf16[384,1536]{1,0:T(8,128)(2,1)} %param.33) | copy-start | bytes 3538948
  576.4 5.2 copy-start.1
  (18 other events, 35.8 us)
Sparse Core Ops, SparseCore 0:
  37.3 38.9 all-gather.5
  122.4 35.4 all-gather.7
  212.1 65.2 all-gather.9
  398.3 62.6 all-gather.11
where the time goes:
time: 596 us; the launch traced here: 588 us
  matrix products  292 us (49%)
  waiting for transfers between devices  207 us (35%)
  local copies, waits for them, and re-layouts  50.2 us (8%)
  between operations  14.8 us (2%)
  other arithmetic  10.6 us (2%)
  starting transfers between devices  6.73 us (1%)
  blocking collectives  6.64 us (1%)
    all_gather x4, waiting for transfers between devices, attn_mlp_block(): kv_all = lax.all_gather(proj_qkv[1:], 'sp', axis=2, tiled=True)  203 us
    sub x2, matrix products, attn_mlp_block(): attn_probs = jax.nn.softmax(scores, axis=-1).astype(jnp.bfloat16)  88.9 us
    dot_general x2, matrix products, attn_mlp_block(): jnp.einsum('chqs,cshk->cqhk', attn_probs, kv_all[1], preferred_element_ty...  78.8 us
    dot_general x4, matrix products, attn_mlp_block(): jnp.einsum('cnf,fd->cnd', up_act, w_down, preferred_element_type=jnp.floa...  62.5 us
    unnamed x75, local copies, waits for them, and re-layouts  27.4 us
    dot_general x4, matrix products, attn_mlp_block(): jnp.einsum('cqhk,hkd->cqd', attended, w_proj, preferred_element_type=jnp....  20.7 us
    dot_general x4, matrix products, attn_mlp_block(): jnp.einsum('cnd,df->cnf', layer_norm(mid_state), w_up, preferred_element_...  19 us
    slice x2, local copies, waits for them, and re-layouts, attn_mlp_block(): kv_all[1]  14 us
  transfers between devices with their start and end apart: 8, of which 6 were waited for; matrix products, arithmetic and copies ran while one was open for 0% of the time, Pallas kernels for 0%

commit v1 on v0

v1 whole, which is shorter than its diff:
```python
import functools
import math

import jax
import jax.numpy as jnp
from jax import lax
from jax.experimental import pallas as pl
from jax.experimental.pallas import tpu as pltpu
from jax.sharding import PartitionSpec as P

F32 = jnp.float32
BF16 = jnp.bfloat16
MESH = pl.DeviceIdType.MESH
VMEM = pl.BlockSpec(memory_space=pltpu.VMEM)
ANY = pl.BlockSpec(memory_space=pl.ANY)

SP = 4
CLIPS = 2
TOK = 768
PATCH = 1536
DIM = 768
ENC_HEADS = 12
HEAD = 64
DDIM = 384
DEC_HEADS = 6
VIS = 96
WIN = 2 * VIS
ROWS = SP * VIS
OWN = 2 * TOK
SEQ = SP * TOK
LAYERS = 2
EXP_SCALE = HEAD ** -0.5 * math.log2(math.e)


def dot(lhs, rhs):
    return jnp.dot(lhs, rhs, preferred_element_type=F32)


def dot_nt(lhs, rhs):
    return lax.dot_general(lhs, rhs, (((1,), (1,)), ((), ())), preferred_element_type=F32)


def dot_tn(lhs, rhs):
    return lax.dot_general(lhs, rhs, (((0,), (0,)), ((), ())), preferred_element_type=F32)


def layer_norm(hidden):
    hid = hidden.astype(F32)
    centred = hid - jnp.mean(hid, axis=-1, keepdims=True)
    var = jnp.mean(centred * centred, axis=-1, keepdims=True)
    return (centred * lax.rsqrt(var + 1e-6)).astype(BF16)


def gelu(val):
    return (0.5 * val * (1.0 + lax.erf(val * math.sqrt(0.5)))).astype(BF16)


def col_max(val):
    return jnp.max(val, axis=0, keepdims=True)


def col_sum(val):
    return jnp.sum(val, axis=0, keepdims=True)


def embed_kernel(mask_ref, patch_ref, pos_ref, wpe_ref, bpe_ref, win_ref, rank_ref, masks, sendbuf, send_sem, recv_sem, mask_send, mask_recv):
    me = lax.axis_index('sp')
    chip = me // 2
    core = me - 2 * chip
    peer = lax.rem(me + 2, SP)
    sib = me + 1 - 2 * core
    diag = lax.rem(sib + 2, SP)

    barrier = pltpu.get_barrier_semaphore()
    for other in (peer, sib, diag):
        pl.semaphore_signal(barrier, inc=1, device_id={'sp': other}, device_id_type=MESH)
    pl.semaphore_wait(barrier, 3)

    mask_copies = []
    for step in range(1, SP):
        copy = pltpu.make_async_remote_copy(
            src_ref=mask_ref, dst_ref=masks.at[step - 1], send_sem=mask_send.at[step - 1], recv_sem=mask_recv.at[step - 1],
            device_id={'sp': lax.rem(me + step, SP)}, device_id_type=MESH)
        copy.start()
        mask_copies.append(copy)
    order_row = lax.broadcasted_iota(jnp.int32, (TOK, TOK), 0)
    order_col = lax.broadcasted_iota(jnp.int32, (TOK, TOK), 1)
    before = jnp.where(order_row < order_col, 1.0, 0.0).astype(BF16)
    for copy in mask_copies:
        copy.wait()

    mine = mask_ref[...].astype(F32)
    others = [masks[k].astype(F32) for k in range(SP - 1)]
    stacked = jnp.concatenate([mine] + others, axis=0)
    local = dot(stacked.astype(BF16), before)
    counts = jnp.sum(stacked, axis=1, keepdims=True)
    dist = lax.broadcasted_iota(jnp.int32, (CLIPS * SP, 1), 0) // CLIPS
    row_dev = lax.rem(me - dist + SP, SP)
    base = jnp.zeros((CLIPS * SP, 1), F32)
    for k in range(SP):
        dev_k = lax.rem(me - k + SP, SP)
        pair = counts[CLIPS * k:CLIPS * k + CLIPS]
        tiled = jnp.concatenate([pair] * SP, axis=0)
        base = base + jnp.where(dev_k < row_dev, tiled, 0.0)
    rank = jnp.where(stacked > 0.0, local + base, float(ROWS))
    rank_ref[...] = rank.astype(jnp.int32)

    def window(clip, mine_rank):
        dest = mine_rank - VIS * me + VIS // 2
        rows = lax.broadcasted_iota(jnp.int32, (WIN, TOK), 0)
        hit = (rows == dest) & (mine_rank < ROWS)
        hit_f32 = jnp.where(hit, 1.0, 0.0)
        select = hit_f32.astype(BF16)
        moved = dot(select, patch_ref[clip]).astype(BF16)
        occupied = jnp.sum(hit_f32, axis=1, keepdims=True)
        emb = dot(moved, wpe_ref[...]) + occupied * bpe_ref[...].astype(F32) + dot(select, pos_ref[...])
        return emb.astype(BF16)

    def send(src, dst, slot, dev):
        copy = pltpu.make_async_remote_copy(
            src_ref=src, dst_ref=dst, send_sem=send_sem.at[slot], recv_sem=recv_sem.at[slot],
            device_id={'sp': dev}, device_id_type=MESH)
        copy.start()
        return copy

    rank_i32 = rank.astype(jnp.int32)
    rank_clip = [rank_i32[0:1], rank_i32[1:2]]
    far = jnp.where(chip == 0, rank_clip[1], rank_clip[0])
    near = jnp.where(chip == 0, rank_clip[0], rank_clip[1])
    sendbuf[...] = window(1 - chip, far)
    to_peer = send(sendbuf, win_ref.at[peer * 0 + me], 0, peer)
    win_ref[me] = window(chip, near)
    to_sib = send(win_ref.at[me], win_ref.at[me], 1, sib)
    to_peer.wait_recv()
    relay = send(win_ref.at[peer], win_ref.at[peer], 2, sib)
    to_sib.wait_recv()
    relay.wait_recv()
    to_peer.wait_send()
    to_sib.wait_send()
    relay.wait_send()


def embed(mask, patches, pos, wpe, bpe):
    return pl.pallas_call(
        embed_kernel,
        out_shape=(jax.ShapeDtypeStruct((SP, WIN, DIM), BF16), jax.ShapeDtypeStruct((CLIPS * SP, TOK), jnp.int32)),
        in_specs=[VMEM] * 5,
        out_specs=(VMEM, VMEM),
        scratch_shapes=[
            pltpu.VMEM((SP - 1, CLIPS, TOK), jnp.int32),
            pltpu.VMEM((WIN, DIM), BF16),
            pltpu.SemaphoreType.DMA((3,)),
            pltpu.SemaphoreType.DMA((3,)),
            pltpu.SemaphoreType.DMA((SP - 1,)),
            pltpu.SemaphoreType.DMA((SP - 1,)),
        ],
        compiler_params=pltpu.CompilerParams(collective_id=0, has_side_effects=True, vmem_limit_bytes=40 * 2 ** 20),
        cost_estimate=pl.CostEstimate(flops=4 * 10 ** 9, bytes_accessed=10 ** 7, transcendentals=0),
        name='embed',
    )(mask, patches, pos, wpe, bpe)


def encoder_kernel(win_ref, token_ref, qkv_hbm, proj_hbm, up_hbm, down_hbm, wed_ref, z_ref, qkv, proj, up, down, hid, norm, q_t, k_n, v_t, o_t, sem):
    copies = []
    for layer in range(LAYERS):
        for idx, (src, dst) in enumerate(((qkv_hbm, qkv), (proj_hbm, proj), (up_hbm, up), (down_hbm, down))):
            copy = pltpu.make_async_copy(src.at[layer], dst.at[layer], sem.at[layer * 4 + idx])
            copy.start()
            copies.append(copy)
    half = VIS // 2
    for blk in range(SP):
        top = win_ref[blk, half:2 * half].astype(F32)
        bottom = win_ref[blk, 2 * half:3 * half].astype(F32)
        if blk > 0:
            top = top + win_ref[blk - 1, 3 * half:].astype(F32)
        if blk < SP - 1:
            bottom = bottom + win_ref[blk + 1, :half].astype(F32)
        hid[blk * VIS:blk * VIS + half] = top.astype(BF16)
        hid[blk * VIS + half:(blk + 1) * VIS] = bottom.astype(BF16)
    for layer in range(LAYERS):
        norm[...] = layer_norm(hid[...])
        copies[layer * 4].wait()
        for part, out in ((0, q_t), (2, v_t)):
            out[...] = dot_nt(qkv[layer, part * DIM:(part + 1) * DIM], norm[...]).astype(BF16)
        k_n[...] = dot_nt(norm[...], qkv[layer, DIM:2 * DIM]).astype(BF16)
        zero = jnp.zeros((HEAD, ROWS), BF16)

        def head_body(pair, carry, layer=layer):
            lanes = pl.ds(pl.multiple_of(pair * 2 * HEAD, 2 * HEAD), 2 * HEAD)
            keys = k_n[:, lanes]
            for odd in range(2):
                rows = pl.ds(pl.multiple_of((2 * pair + odd) * HEAD, HEAD), HEAD)
                q_head = q_t[rows, :]
                q_pad = jnp.concatenate([zero, q_head] if odd else [q_head, zero], axis=0)
                scores = dot(keys, q_pad)
                e = jnp.exp2(scores * EXP_SCALE - col_max(scores) * EXP_SCALE)
                o = dot(v_t[rows, :], e.astype(BF16))
                o_t[rows, :] = (o * (1.0 / col_sum(e))).astype(BF16)
            return carry

        lax.fori_loop(0, ENC_HEADS // 2, head_body, 0)
        copies[layer * 4 + 1].wait()
        mid = (hid[...].astype(F32) + dot_tn(o_t[...], proj[layer])).astype(BF16)
        hid[...] = mid
        norm[...] = layer_norm(mid)
        copies[layer * 4 + 2].wait()
        copies[layer * 4 + 3].wait()
        acc = None
        step = DIM
        for lo in range(0, 4 * DIM, step):
            act = gelu(dot(norm[...], up[layer, :, lo:lo + step]))
            part = dot(act, down[layer, lo:lo + step, :])
            acc = part if acc is None else acc + part
        hid[...] = (mid.astype(F32) + acc).astype(BF16)
    z_ref[:ROWS] = dot(layer_norm(hid[...]), wed_ref[...]).astype(BF16)
    first = lax.broadcasted_iota(jnp.int32, (2 * HEAD, DDIM), 0) == 0
    z_ref[ROWS:] = jnp.where(first, token_ref[...].astype(F32), 0.0).astype(BF16)


def encode(win, token, qkv_t, proj, up, down, wed):
    return pl.pallas_call(
        encoder_kernel,
        out_shape=jax.ShapeDtypeStruct((ROWS + 2 * HEAD, DDIM), BF16),
        in_specs=[VMEM, VMEM, ANY, ANY, ANY, ANY, VMEM],
        out_specs=VMEM,
        scratch_shapes=[
            pltpu.VMEM((LAYERS, 3 * DIM, DIM), BF16),
            pltpu.VMEM((LAYERS, DIM, DIM), BF16),
            pltpu.VMEM((LAYERS, DIM, 4 * DIM), BF16),
            pltpu.VMEM((LAYERS, 4 * DIM, DIM), BF16),
            pltpu.VMEM((ROWS, DIM), BF16),
            pltpu.VMEM((ROWS, DIM), BF16),
            pltpu.VMEM((DIM, ROWS), BF16),
            pltpu.VMEM((ROWS, DIM), BF16),
            pltpu.VMEM((DIM, ROWS), BF16),
            pltpu.VMEM((DIM, ROWS), BF16),
            pltpu.SemaphoreType.DMA((LAYERS * 4,)),
        ],
        compiler_params=pltpu.CompilerParams(vmem_limit_bytes=56 * 2 ** 20),
        cost_estimate=pl.CostEstimate(flops=12 * 10 ** 9, bytes_accessed=3 * 10 ** 7, transcendentals=0),
        name='encoder',
    )(win, token, qkv_t, proj, up, down, wed)


Q_BLK = 256
K_BLK = 128
CHUNK = 256
Q_BLKS = OWN // Q_BLK
UNITS = DEC_HEADS * Q_BLKS


def decoder_layer(hid, other_norm, wqkv, wproj, wup, wdown, norm, q_z, k_n, v_t, o_t, s_even, s_odd, finish):
    def norm_body(i, carry):
        rows = pl.ds(pl.multiple_of(i * CHUNK, CHUNK), CHUNK)
        norm[rows, :] = layer_norm(hid[rows, :])
        return carry

    lax.fori_loop(0, OWN // CHUNK, norm_body, 0)
    other_norm()

    def q_body(i, carry):
        rows = pl.ds(pl.multiple_of(i * CHUNK, CHUNK), CHUNK)
        q = dot_nt(wqkv[0:DDIM], norm[rows, :]).astype(BF16)
        zero = jnp.zeros((HEAD, CHUNK), BF16)
        for head in range(DEC_HEADS):
            q_head = q[head * HEAD:(head + 1) * HEAD]
            lo, hi = (q_head, zero) if head % 2 == 0 else (zero, q_head)
            q_z[head, 0:HEAD, rows] = lo
            q_z[head, HEAD:2 * HEAD, rows] = hi
        return carry

    lax.fori_loop(0, OWN // CHUNK, q_body, 0)

    def kv_body(i, carry):
        rows = pl.ds(pl.multiple_of(i * CHUNK, CHUNK), CHUNK)
        a = norm[rows, :]
        k_n[rows, :] = dot_nt(a, wqkv[DDIM:2 * DDIM]).astype(BF16)
        v_t[:, rows] = dot_nt(wqkv[2 * DDIM:3 * DDIM], a).astype(BF16)
        return carry

    lax.fori_loop(0, SEQ // CHUNK, kv_body, 0)

    def place(unit):
        head = unit // Q_BLKS
        return head, pl.ds(pl.multiple_of((unit - head * Q_BLKS) * Q_BLK, Q_BLK), Q_BLK)

    def mixed(unit_q, s_q, unit_p, s_p, max8):
        if unit_q is not None:
            head_q, cols_q = place(unit_q)
            q = q_z[head_q, :, cols_q]
            lanes = pl.ds(pl.multiple_of((head_q // 2) * 2 * HEAD, 2 * HEAD), 2 * HEAD)
        if unit_p is not None:
            head_p, cols_p = place(unit_p)
            shift = col_max(max8) * EXP_SCALE
            v_rows = pl.ds(pl.multiple_of(head_p * HEAD, HEAD), HEAD)
        new_max = total = acc = None
        for lo in range(0, SEQ, K_BLK):
            if unit_q is not None:
                s = dot(k_n[lo:lo + K_BLK, lanes], q)
                s_q[lo:lo + K_BLK, :] = s
                m = jnp.max(s.reshape(K_BLK // 8, 8, Q_BLK), axis=0)
                new_max = m if new_max is None else jnp.maximum(new_max, m)
            if unit_p is not None:
                e = jnp.exp2(s_p[lo:lo + K_BLK, :] * EXP_SCALE - shift)
                t = jnp.sum(e.reshape(K_BLK // 8, 8, Q_BLK), axis=0)
                total = t if total is None else total + t
                o = dot(v_t[v_rows, lo:lo + K_BLK], e.astype(BF16))
                acc = o if acc is None else acc + o
        if unit_p is not None:
            o_t[v_rows, cols_p] = (acc * (1.0 / col_sum(total))).astype(BF16)
        return new_max

    first = mixed(0, s_even, None, None, None)

    def attn_body(i, max8):
        unit = 2 * i
        max_odd = mixed(unit + 1, s_odd, unit, s_even, max8)
        return mixed(jnp.minimum(unit + 2, UNITS - 1), s_even, unit + 1, s_odd, max_odd)

    lax.fori_loop(0, UNITS // 2, attn_body, first)

    def mlp_body(i, carry):
        rows = pl.ds(pl.multiple_of(i * CHUNK, CHUNK), CHUNK)
        mid = (hid[rows, :].astype(F32) + dot_tn(o_t[:, rows], wproj[...])).astype(BF16)
        act = gelu(dot(layer_norm(mid), wup[...]))
        finish(rows, (mid.astype(F32) + dot(act, wdown[...])).astype(BF16))
        return carry

    lax.fori_loop(0, OWN // CHUNK, mlp_body, 0)


def first_layer_kernel(z_ref, rank_ref, pos_ref, wqkv, wproj, wup, wdown, out_ref, hid, norm, *scratch):
    me = lax.axis_index('sp')
    chip = me // 2
    core = me - 2 * chip
    peer = lax.rem(me + 2, SP)
    sib = me + 1 - 2 * core
    diag = lax.rem(sib + 2, SP)

    def tokens(dev):
        slot = lax.rem(me - dev + SP, SP)
        rank = rank_ref[pl.ds(2 * slot + chip, 1), :]
        rank_col = jnp.transpose(jnp.broadcast_to(rank.astype(F32), (8, TOK)))[:, 0:1]
        lanes = lax.broadcasted_iota(jnp.int32, (TOK, ROWS + 2 * HEAD), 1).astype(F32)
        select = jnp.where(lanes == rank_col, 1.0, 0.0).astype(BF16)
        return (dot(select, z_ref[...]) + pos_ref[slot].astype(F32)).astype(BF16)

    hid[0:TOK] = tokens(peer)
    hid[TOK:OWN] = tokens(me)

    def other_norm():
        norm[OWN:OWN + TOK] = layer_norm(tokens(diag))
        norm[OWN + TOK:SEQ] = layer_norm(tokens(sib))

    def finish(rows, val):
        out_ref[rows, :] = val

    decoder_layer(hid, other_norm, wqkv, wproj, wup, wdown, norm, *scratch, finish)


def last_layer_kernel(hid, other, wqkv, wproj, wup, wdown, out_ref, norm, *scratch):
    def other_norm():
        def body(i, carry):
            rows = pl.ds(pl.multiple_of(i * CHUNK, CHUNK), CHUNK)
            norm[pl.ds(pl.multiple_of(OWN + i * CHUNK, CHUNK), CHUNK), :] = layer_norm(other[rows, :])
            return carry

        lax.fori_loop(0, OWN // CHUNK, body, 0)

    def finish(rows, val):
        out_ref[rows, :] = layer_norm(val)

    decoder_layer(hid, other_norm, wqkv, wproj, wup, wdown, norm, *scratch, finish)


LAYER_SCRATCH = [
    pltpu.VMEM((SEQ, DDIM), BF16),
    pltpu.VMEM((DEC_HEADS, 2 * HEAD, OWN), BF16),
    pltpu.VMEM((SEQ, DDIM), BF16),
    pltpu.VMEM((DDIM, SEQ), BF16),
    pltpu.VMEM((DDIM, OWN), BF16),
    pltpu.VMEM((SEQ, Q_BLK), F32),
    pltpu.VMEM((SEQ, Q_BLK), F32),
]
LAYER_COST = pl.CostEstimate(flops=30 * 10 ** 9, bytes_accessed=10 ** 7, transcendentals=3 * 10 ** 7)


def first_layer(z, rank, pos, wqkv, wproj, wup, wdown):
    return pl.pallas_call(
        first_layer_kernel,
        out_shape=jax.ShapeDtypeStruct((OWN, DDIM), BF16),
        in_specs=[VMEM] * 7,
        out_specs=VMEM,
        scratch_shapes=[pltpu.VMEM((OWN, DDIM), BF16)] + LAYER_SCRATCH,
        compiler_params=pltpu.CompilerParams(vmem_limit_bytes=50 * 2 ** 20),
        cost_estimate=LAYER_COST,
        name='decoder_first',
    )(z, rank, pos, wqkv, wproj, wup, wdown)


def last_layer(hid, other, wqkv, wproj, wup, wdown):
    return pl.pallas_call(
        last_layer_kernel,
        out_shape=jax.ShapeDtypeStruct((OWN, DDIM), BF16),
        in_specs=[VMEM] * 6,
        out_specs=VMEM,
        scratch_shapes=LAYER_SCRATCH,
        compiler_params=pltpu.CompilerParams(vmem_limit_bytes=50 * 2 ** 20),
        cost_estimate=LAYER_COST,
        name='decoder_last',
    )(hid, other, wqkv, wproj, wup, wdown)


def solution(mesh):
    across = [(0, 2), (1, 3), (2, 0), (3, 1)]
    beside = [(0, 1), (1, 0), (2, 3), (3, 2)]

    def local_program(patches, vis_mask, enc_pos, dec_pos, w_pe, b_pe, enc_qkv, enc_proj, enc_up, enc_down, w_ed, mask_token, dec_qkv, dec_proj, dec_up, dec_down, w_out):
        me = lax.axis_index('sp')
        chip = me // 2
        enc_qkv_t = jnp.transpose(enc_qkv, (0, 2, 3, 4, 1)).reshape(LAYERS, 3 * DIM, DIM)
        dec_qkv_t = jnp.transpose(dec_qkv, (0, 2, 3, 4, 1)).reshape(LAYERS, 3 * DDIM, DDIM)
        enc_proj2 = enc_proj.reshape(LAYERS, DIM, DIM)
        dec_proj2 = dec_proj.reshape(LAYERS, DDIM, DDIM)
        win, rank = embed(vis_mask, patches, enc_pos, w_pe, b_pe.reshape(1, DIM))
        dec_pos, win = lax.optimization_barrier((dec_pos, win))
        pos_peer = lax.ppermute(dec_pos, 'sp', across)
        pos_sib = lax.ppermute(dec_pos, 'sp', beside)
        pos_diag = lax.ppermute(pos_peer, 'sp', beside)
        even = me == 2 * chip
        pos = jnp.stack([dec_pos, jnp.where(even, pos_diag, pos_sib), pos_peer, jnp.where(even, pos_sib, pos_diag)])
        z = encode(win, mask_token.reshape(1, DDIM), enc_qkv_t, enc_proj2, enc_up, enc_down, w_ed)
        hid = first_layer(z, rank, pos, dec_qkv_t[0], dec_proj2[0], dec_up[0], dec_down[0])
        other = lax.ppermute(hid, 'sp', beside)
        final = last_layer(hid, other, dec_qkv_t[1], dec_proj2[1], dec_up[1], dec_down[1])
        back = lax.ppermute(final[:TOK], 'sp', across)
        here = final[TOK:]
        both = jnp.stack([jnp.where(chip == 0, here, back), jnp.where(chip == 0, back, here)])
        return jnp.einsum('cne,ep->cnp', both, w_out, preferred_element_type=F32)

    row_spec = P('dp', 'sp', None)
    pos_spec = P(('dp', 'sp'), None)
    arg_specs = (row_spec, P('dp', 'sp'), pos_spec, pos_spec) + (P(),) * 13
    return jax.shard_map(local_program, mesh=mesh, in_specs=arg_specs, out_specs=row_spec, check_vma=False)
```

time: 596 us -> 206 us (0.35); the launches traced: 588 us -> 205 us
  matrix products: 292 us -> 5.14 us
  waiting for transfers between devices: 207 us -> 16.3 us
  Pallas kernels: 0 us -> 158 us
  local copies, waits for them, and re-layouts: 50.2 us -> 17.2 us
  between operations: 14.8 us -> 0.14 us
  blocking collectives: 6.64 us -> 0 us
    all_gather x4 -> x0, waiting for transfers between devices: 203 us -> none  [attn_mlp_block(): kv_all = lax.all_gather(proj_qkv[1:], 'sp', axis=2, tiled=True)]
    dot_general x25 -> x1, matrix products: 204 us -> 5.14 us  [local_program(): return jnp.einsum('cne,ep->cnp', both, w_out, preferred_element_type=F32)]
    pallas_call x0 -> x4, Pallas kernels: none -> 158 us  [the longest x1 55.5 us: first_layer(): pl.pallas_call(first_layer_kernel, out_shape=jax.ShapeDtypeStruct((OWN, D...]
    sub x2 -> x0, matrix products: 88.9 us -> none  [attn_mlp_block(): attn_probs = jax.nn.softmax(scores, axis=-1).astype(jnp.bfloat16)]
    slice x11 -> x3, local copies, waits for them, and re-layouts: 21.7 us -> 2.07 us  [the longest x1 1.22 us: local_program(): dec_qkv_t[1]]
    unnamed x75 -> x32, local copies, waits for them, and re-layouts: 27.4 us -> 9.37 us
    ppermute x4 -> x5, waiting for transfers between devices: 4.2 us -> 16.3 us  [the longest x1 13.9 us: local_program(): back = lax.ppermute(final[:TOK], 'sp', across)]
    unnamed x1 -> x0, blocking collectives: 6.64 us -> none
  transfers between devices with their start and end apart: 8 -> 5, of which waited for: 6 -> 2; matrix products, arithmetic and copies ran while one was open for 0% -> 3% of each run, Pallas kernels for 0% -> 15%
where the time goes in v1:
time: 206 us; the launch traced here: 205 us
  Pallas kernels  158 us (77%)
  local copies, waits for them, and re-layouts  17.2 us (8%)
  waiting for transfers between devices  16.3 us (8%)
  other arithmetic  5.66 us (3%)
  matrix products  5.14 us (2%)
  starting transfers between devices  2.99 us (1%)
    pallas_call x1, Pallas kernels, first_layer(): pl.pallas_call(first_layer_kernel, out_shape=jax.ShapeDtypeStruct((OWN, D...  55.5 us
    pallas_call x1, Pallas kernels, last_layer(): pl.pallas_call(last_layer_kernel, out_shape=jax.ShapeDtypeStruct((OWN, DD...  54.5 us
    pallas_call x1, Pallas kernels, encode(): pl.pallas_call(encoder_kernel, out_shape=jax.ShapeDtypeStruct((ROWS + 2 *...  30.6 us
    pallas_call x1, Pallas kernels, embed(): pl.pallas_call(embed_kernel, out_shape=(jax.ShapeDtypeStruct((SP, WIN, DI...  17.4 us
    ppermute x1, waiting for transfers between devices, local_program(): back = lax.ppermute(final[:TOK], 'sp', across)  13.9 us
    unnamed x32, local copies, waits for them, and re-layouts  9.37 us
    dot_general x1, matrix products, local_program(): return jnp.einsum('cne,ep->cnp', both, w_out, preferred_element_type=F32)  5.14 us
    another operation x2, other arithmetic, local_program(): jnp.stack([dec_pos, jnp.where(even, pos_diag, pos_sib), pos_peer, jnp.whe...  4.48 us
  transfers between devices with their start and end apart: 5, of which 2 were waited for; matrix products, arithmetic and copies ran while one was open for 3% of the time, Pallas kernels for 15%

profile of v1, /device:TPU:0, one launch (start us, length us, event | category | flops | bytes accessed | tf_op | source)
XLA Modules:
  0.0 205.5 jit_solution(12512947898235995279)
XLA Ops:
  0.0 0.8 reshape.22.bpe_ref
  0.8 2.3 %copy-done.3 = bf16[2,768,1536]{2,1,0:T(8,128)(2,1)S(1)} copy-done((bf16[2,768,1536]{2,1,0:T(8,128)(2,1)S(1)}, bf16[2,768,1536]{2,1,0:T(8,128)(2,1)}, u32[]{:S(2)}) %copy-start.3) | copy-done | bytes 4718616
  3.1 1.7 copy-done.4
  4.8 1.3 copy-done.5
  6.1 0.7 copy-done.6
  6.8 17.4 %embed.1 = (bf16[4,192,768]{2,1,0:T(8,128)(2,1)S(1)}, s32[8,768]{1,0:T(8,128)S(1)}) custom-call(s32[2,768]{1,0:T(2,128)S(1)} %copy-done.6, bf16[2,768,1536]{2,1,0:T(8,128)(2,1)S(1)} %copy-done.3, bf16[768,768]{1,0:T(8,128)(2,1)S(1)} %copy-done.5, bf16[1536,768]{1,0:T(8,128)(2,1)S(1)} %copy-done.4, bf16[1,768]{1,0:T(2,128)(2,1)S(1)} %reshape.22.bpe_ref), custom_call_target="tpu_custom_call" | custom-call | flops 4000000000 | bytes 10000000 | tf_op jit(solution)/shard_map/embed/pallas_call | solution.py:144
  24.2 1.0 copy-done.7
  25.2 0.6 copy-done.9
  26.8 30.6 %encoder.1.z_ref = bf16[512,384]{1,0:T(8,128)(2,1)} custom-call(bf16[4,192,768]{2,1,0:T(8,128)(2,1)} %copy-done.7, bf16[1,384]{1,0:T(2,128)(2,1)} %reshape.23.token_ref, bf16[2,2304,768]{2,1,0:T(8,128)(2,1)} %bitcast.35, bf16[2,768,768]{2,1,0:T(8,128)(2,1)} %bitcast.36, bf16[2,768,3072]{2,1,0:T(8,128)(2,1)} %up_hbm.1, bf16[2,3072,768]{2,1,0:T(8,128)(2,1)} %down_hbm.1, ...), custom_call_target="tpu_custom_call" | custom-call | flops 12000000000 | bytes 30000000 | tf_op jit(solution)/shard_map/encoder/pallas_call | solution.py:221
  57.4 1.2 fusion.6
  58.6 0.8 copy-done.11
  59.4 1.2 slice_bitcast_fusion.1
  60.7 0.8 fusion.7
  61.5 3.2 %slice_bitcast_fusion = (bf16[1536,384]{1,0:T(8,128)(2,1)}, bf16[1536,384]{1,0:T(8,128)(2,1)}) fusion(bf16[2,1536,384]{2,1,0:T(8,128)(2,1)} %param.32), kind=kLoop, calls=%fused_computation.6 | loop fusion | bytes 4718592 | tf_op jit(solution)/shard_map/squeeze | solution.py:435
  64.7 1.4 select_bitcast_fusion.3
  66.1 3.1 %pad_maximum_fusion.pos_ref = bf16[4,768,384]{2,1,0:T(8,128)(2,1)} fusion(bf16[1,768,384]{2,1,0:T(8,128)(2,1)S(1)} %get-tuple-element.22, bf16[1,768,384]{2,1,0:T(8,128)(2,1)} %bitcast.5, bf16[1,768,384]{2,1,0:T(8,128)(2,1)S(1)} %get-tuple-element.21, bf16[1,768,384]{2,1,0:T(8,128)(2,1)} %bitcast.3), kind=kLoop, calls=%fused_computation | loop fusion | flops 3538944 | bytes 4718592 | tf_op jit(solution)/shard_map/stack | solution.py:431
  69.3 55.5 %decoder_first.1.hid = bf16[1536,384]{1,0:T(8,128)(2,1)S(1)} custom-call(bf16[512,384]{1,0:T(8,128)(2,1)S(1)} %copy-done.8, s32[8,768]{1,0:T(8,128)S(1)} %copy-done.10, bf16[4,768,384]{2,1,0:T(8,128)(2,1)} %pad_maximum_fusion.pos_ref, bf16[1152,384]{1,0:T(8,128)(2,1)S(1)} %bitcast.31, bf16[384,384]{1,0:T(8,128)(2,1)S(1)} %bitcast.33, ...), custom_call_target="tpu_custom_call" | custom-call | flops 30000001024 | bytes 10000000 | tf_op jit(solution)/shard_map/decoder_first/pallas_call | solution.py:389
  125.2 2.5 %collective-permute-done.3.other = bf16[1536,384]{1,0:T(8,128)(2,1)S(1)} collective-permute-done((bf16[1536,384]{1,0:T(8,128)(2,1)S(1)}, bf16[1536,384]{1,0:T(8,128)(2,1)S(1)}, u32[]{:S(2)}, u32[]{:S(2)}) %collective-permute-start.3) | collective-permute-done | bytes 1179680 | tf_op jit(solution)/shard_map/ppermute | solution.py:434
  127.6 1.0 copy-done.15
  128.7 54.5 %decoder_last.1 = bf16[1536,384]{1,0:T(8,128)(2,1)S(1)} custom-call(bf16[1536,384]{1,0:T(8,128)(2,1)S(1)} %decoder_first.1.hid, bf16[1536,384]{1,0:T(8,128)(2,1)} %copy-done.15, bf16[1152,384]{1,0:T(8,128)(2,1)S(1)} %bitcast.30, bf16[384,384]{1,0:T(8,128)(2,1)S(1)} %bitcast.32, bf16[384,1536]{1,0:T(8,128)(2,1)} %get-tuple-element.15.wup, ...), custom_call_target="tpu_custom_call" | custom-call | flops 30000001024 | bytes 10000000 | tf_op jit(solution)/shard_map/decoder_last/pallas_call | solution.py:402
  183.2 2.1 %collective-permute-start.4 = (bf16[768,384]{1,0:T(8,128)(2,1)S(1)}, bf16[768,384]{1,0:T(8,128)(2,1)}, u32[]{:S(2)}, u32[]{:S(2)}) collective-permute-start(bf16[768,384]{1,0:T(8,128)(2,1)S(1)} %slice.47), channel_id=1, source_target_pairs={{0,2},{1,3},{2,0},{3,1},{4,6},{5,7},{6,4},{7,5},{8,10},{9,11},{10,... | collective-permute-start | bytes 1769480 | tf_op jit(solution)/shard_map/ppermute | solution.py:436
  185.2 13.9 %collective-permute-done.4 = bf16[768,384]{1,0:T(8,128)(2,1)} collective-permute-done((bf16[768,384]{1,0:T(8,128)(2,1)S(1)}, bf16[768,384]{1,0:T(8,128)(2,1)}, u32[]{:S(2)}, u32[]{:S(2)}) %collective-permute-start.4) | collective-permute-done | bytes 589856 | tf_op jit(solution)/shard_map/ppermute | solution.py:436
  199.1 1.2 select_bitcast_fusion.1
  200.3 5.1 %fusion = f32[2,768,1536]{2,1,0:T(8,128)} fusion(bf16[1,768,384]{2,1,0:T(8,128)(2,1)S(1)} %get-tuple-element.18, bf16[1,768,384]{2,1,0:T(8,128)(2,1)S(1)} %get-tuple-element.17, bf16[384,1536]{1,0:T(8,128)(2,1)S(1)} %copy-done), kind=kOutput, calls=%fused_computation.1 | convolution fusion | flops 1812529152 | bytes 11796480 | tf_op jit(solution)/shard_map/cne,ep->cnp/dot_general | solution.py:439
  (33 shorter events, 1.6 us)
Async XLA Ops:
  0.0 200.3 %copy-start = (bf16[384,1536]{1,0:T(8,128)(2,1)S(1)}, bf16[384,1536]{1,0:T(8,128)(2,1)}, u32[]{:S(2)}) copy-start(bf16[384,1536]{1,0:T(8,128)(2,1)} %param.33) | copy-start | bytes 3538948
  0.8 2.3 %copy-start.3 = (bf16[2,768,1536]{2,1,0:T(8,128)(2,1)S(1)}, bf16[2,768,1536]{2,1,0:T(8,128)(2,1)}, u32[]{:S(2)}) copy-start(bf16[2,768,1536]{2,1,0:T(8,128)(2,1)} %patch_ref.1) | copy-start | bytes 14155780
  3.1 1.7 copy-start.4
  4.8 1.3 copy-start.5
  6.1 0.7 copy-start.6
  6.8 19.4 %copy-start.14 = (bf16[384]{0:T(512)(128)(2,1)S(1)}, bf16[384]{0:T(512)(128)(2,1)}, u32[]{:S(2)}) copy-start(bf16[384]{0:T(512)(128)(2,1)} %param.28) | copy-start | bytes 2308
  24.2 1.0 copy-start.7
  25.2 0.6 copy-start.9
  25.8 38.9 %collective-permute-start.2 = (bf16[768,384]{1,0:T(8,128)(2,1)}, bf16[768,384]{1,0:T(8,128)(2,1)}, u32[]{:S(2)}, u32[]{:S(2)}) collective-permute-start(bf16[768,384]{1,0:T(8,128)(2,1)} %param.20), channel_id=1, source_target_pairs={{0,1},{1,0},{2,3},{3,2},{4,5},{5,4},{6,7},{7,6},{8,9},{9,8},{10,11... | collective-permute-start | bytes 1769480 | tf_op jit(solution)/shard_map/ppermute | solution.py:428
  26.2 34.4 %collective-permute-start = (bf16[768,384]{1,0:T(8,128)(2,1)}, bf16[768,384]{1,0:T(8,128)(2,1)}, u32[]{:S(2)}, u32[]{:S(2)}) collective-permute-start(bf16[768,384]{1,0:T(8,128)(2,1)} %param.20), channel_id=1, source_target_pairs={{0,2},{1,3},{2,0},{3,1},{4,6},{5,7},{6,4},{7,5},{8,10},{9,11},{10,... | collective-permute-start | bytes 1769480 | tf_op jit(solution)/shard_map/ppermute | solution.py:427
  26.8 30.6 %copy-start.12 = (bf16[2,384,3,6,64]{1,4,3,2,0:T(8,128)(2,1)S(1)}, bf16[2,384,3,6,64]{1,4,3,2,0:T(8,128)(2,1)}, u32[]{:S(2)}) copy-start(bf16[2,384,3,6,64]{1,4,3,2,0:T(8,128)(2,1)} %param.29) | copy-start | bytes 5308420
  57.4 2.0 copy-start.11
  59.4 1.3 copy-start.13
  60.6 4.2 %collective-permute-start.1 = (bf16[768,384]{1,0:T(8,128)(2,1)}, bf16[768,384]{1,0:T(8,128)(2,1)}, u32[]{:S(2)}, u32[]{:S(2)}) collective-permute-start(bf16[768,384]{1,0:T(8,128)(2,1)} %collective-permute-done), channel_id=1, source_target_pairs={{0,1},{1,0},{2,3},{3,2},{4,5},{5,4},{6,7},{7,6},{8,9},{9,8},{10,11... | collective-permute-start | bytes 1769480 | tf_op jit(solution)/shard_map/ppermute | solution.py:429
  66.1 3.2 %copy-start.1 = (bf16[1,3,6,64,384]{4,3,2,1,0:T(8,128)(2,1)S(1)}, bf16[1,3,6,64,384]{4,3,2,1,0:T(8,128)(2,1)}, u32[]{:S(2)}) copy-start(bf16[1,3,6,64,384]{4,3,2,1,0:T(8,128)(2,1)} %get-tuple-element.20) | copy-start | bytes 2654212
  66.1 3.2 %copy-start.2 = (bf16[1,6,64,384]{3,2,1,0:T(8,128)(2,1)S(1)}, bf16[1,6,64,384]{3,2,1,0:T(8,128)(2,1)}, u32[]{:S(2)}) copy-start(bf16[1,6,64,384]{3,2,1,0:T(8,128)(2,1)} %get-tuple-element.24) | copy-start | bytes 884740
  66.1 3.1 %copy-start.8 = (bf16[512,384]{1,0:T(8,128)(2,1)S(1)}, bf16[512,384]{1,0:T(8,128)(2,1)}, u32[]{:S(2)}) copy-start(bf16[512,384]{1,0:T(8,128)(2,1)} %encoder.1.z_ref) | copy-start | bytes 1179652
  66.1 3.1 %copy-start.10 = (s32[8,768]{1,0:T(8,128)S(1)}, s32[8,768]{1,0:T(8,128)}, u32[]{:S(2)}) copy-start(s32[8,768]{1,0:T(8,128)} %copy-done.9) | copy-start | bytes 73732
  124.7 2.9 %collective-permute-start.3 = (bf16[1536,384]{1,0:T(8,128)(2,1)S(1)}, bf16[1536,384]{1,0:T(8,128)(2,1)S(1)}, u32[]{:S(2)}, u32[]{:S(2)}) collective-permute-start(bf16[1536,384]{1,0:T(8,128)(2,1)S(1)} %decoder_first.1.hid), channel_id=1, source_target_pairs={{0,1},{1,0},{2,3},{3,2},{4,5},{5,4},{6,7},{7,6},{8,9},{9,8},{10,11... | collective-permute-start | bytes 3538952 | tf_op jit(solution)/shard_map/ppermute | solution.py:434
  127.6 1.0 copy-start.15
  183.2 15.9 %collective-permute-start.4 = (bf16[768,384]{1,0:T(8,128)(2,1)S(1)}, bf16[768,384]{1,0:T(8,128)(2,1)}, u32[]{:S(2)}, u32[]{:S(2)}) collective-permute-start(bf16[768,384]{1,0:T(8,128)(2,1)S(1)} %slice.47), channel_id=1, source_target_pairs={{0,2},{1,3},{2,0},{3,1},{4,6},{5,7},{6,4},{7,5},{8,10},{9,11},{10,... | collective-permute-start | bytes 1769480 | tf_op jit(solution)/shard_map/ppermute | solution.py:436
